TPU v7x, 32 devices: a whole 2x2x4 slice. The times are simulated.
32 devices in a mesh: feat: 8 (over z, y), row: 2 (over x), col: 2 (over core).
Axes of the slice: x: 2, y: 2, z: 4, core: 2. Of those that a mesh axis runs over, the one named last changes fastest.
Arguments:
- local_x: float32 [4, 32, 256], P(('row', 'col'), 'feat'), may hold values from -4 to 4
- dual_var: float32 [4, 32, 256], P(('row', 'col'), 'feat'), may hold values from -2 to 2
- consensus_old: float32 [32, 256], P('feat'), may hold values from -4 to 4
- blocks_data: bfloat16 [4, 32, 512, 256], P(('row', 'col'), 'feat'), may hold values from -0.375 to 0.375
- row_index: int32 [4, 32, 512], P(('row', 'col'), 'feat'), may hold values from 0 to 16383, as said below
- labels: int32 [4, 16384], P(('row', 'col')), may hold values 0 or 1
Outputs:
- solved_x: float32 [4, 32, 256], P(('row', 'col'), 'feat')
- dual_new: float32 [4, 32, 256], P(('row', 'col'), 'feat')
- consensus: float32 [32, 256], P('feat')
- norms: float32 [2], replicated
Inputs may be any that keep to these rules, and one draw needn't show every extreme that they name: `row_index`: the 512 rows of one block are distinct samples of its shard; a sample may appear in no block or in several.
All inputs are finite; a program needn't handle non-finite values. No bound on the sum of `labels` on one device may be relied on, other than what follows from the above.
Results may differ from a plain program's by a relative error of at most 0.0019.
Values sent between devices are 32-bit elements; how exact they have to be, the bound alone decides.
A program may use at most 64 MiB of HBM per device.

v0:
```python
import jax
import jax.numpy as jnp
from jax import lax
from jax.sharding import PartitionSpec as P

NEWTON_STEPS = 2
CG_STEPS = 3
penalty = 1.0
damping = 0.5
threshold = 0.05


def shrink(values):
    return jnp.sign(values) * jnp.maximum(jnp.abs(values) - threshold, 0.0)


def conjugate_solve(hessian, gradient):
    delta = jnp.zeros_like(gradient)
    residual = gradient
    direction = gradient
    power = jnp.sum(residual * residual, axis=1)
    for cg_step in range(CG_STEPS):
        image = jnp.einsum("bkl,bl->bk", hessian, direction, precision=lax.Precision.HIGHEST)
        alpha = power / jnp.sum(direction * image, axis=1)
        delta = delta + alpha[:, None] * direction
        residual = residual - alpha[:, None] * image
        power_next = jnp.sum(residual * residual, axis=1)
        direction = residual + (power_next / power)[:, None] * direction
        power = power_next
    return delta


def local(local_x, dual_var, consensus_old, blocks_data, row_index, labels):
    iterate = local_x[0]
    dual_local = dual_var[0]
    block_rows = blocks_data[0]
    index_rows = row_index[0]
    targets = labels[0].astype(jnp.float32)
    samples = targets.shape[0]
    target = consensus_old - dual_local
    flat_index = index_rows.reshape(-1)
    identity = jnp.eye(iterate.shape[1], dtype=jnp.float32)
    for newton_step in range(NEWTON_STEPS):
        rounded = iterate.astype(jnp.bfloat16)
        partial_value = jnp.einsum(
            "brk,bk->br", block_rows, rounded, preferred_element_type=jnp.float32
        )
        local_margins = jax.ops.segment_sum(
            partial_value.reshape(-1), flat_index, num_segments=samples
        )
        margins = lax.psum(local_margins, "feat")
        prob = jax.nn.sigmoid(margins)
        misfit = prob - targets
        weights = prob * (1.0 - prob)
        misfit_rows = misfit[index_rows].astype(jnp.bfloat16)
        gradient = jnp.einsum(
            "brk,br->bk", block_rows, misfit_rows, preferred_element_type=jnp.float32
        )
        gradient = gradient + penalty * (iterate - target)
        weighted = (block_rows * weights[index_rows][:, :, None]).astype(jnp.bfloat16)
        hessian = (
            jnp.einsum("brk,brl->bkl", block_rows, weighted, preferred_element_type=jnp.float32)
            + penalty * identity
        )
        delta = conjugate_solve(hessian, gradient)
        iterate = iterate - damping * delta
    shards = lax.axis_size(("row", "col"))
    combined = iterate + dual_local
    totals = lax.psum(combined, ("row", "col"))
    consensus = shrink(totals / jnp.float32(shards))
    dual_next = dual_local + iterate - consensus
    primal_local = jnp.sum((iterate - consensus) ** 2)
    change_local = jnp.sum((consensus - consensus_old) ** 2)
    primal_total, change_total = lax.psum(
        (primal_local, change_local / jnp.float32(shards)), ("feat", "row", "col")
    )
    norms = jnp.stack(
        [jnp.sqrt(primal_total), penalty * jnp.sqrt(jnp.float32(shards) * change_total)]
    )
    return (iterate[None], dual_next[None], consensus, norms)


def solution(mesh):
    placed = (
        P(("row", "col"), "feat", None),
        P(("row", "col"), "feat", None),
        P("feat", None),
        P(("row", "col"), "feat", None, None),
        P(("row", "col"), "feat", None),
        P(("row", "col"), None),
    )
    return jax.shard_map(
        local,
        mesh=mesh,
        in_specs=placed,
        out_specs=(
            P(("row", "col"), "feat", None),
            P(("row", "col"), "feat", None),
            P("feat", None),
            P(),
        ),
        check_vma=False,
    )
```

profile of v0, /device:TPU:0, one launch (start us, length us, event | category | flops | bytes accessed | tf_op | source)
XLA Modules:
  0.0 292.5 jit_solution(3661908139111151564)
XLA Ops:
  7.2 0.7 fusion.62
  7.9 1.6 fusion.26
  9.6 11.8 %scatter_custom_fusion = f32[16384]{0:T(1024)} fusion(s32[2048]{0:T(1024)S(1)} %bitcast.146, f32[2048]{0:T(1024)S(1)} %bitcast.149, f32[]{:T(128)} %constant.9.clone.1), kind=kCustom, calls=%fused_computation.36 | custom fusion | flops 2048 | bytes 65540 | tf_op jit(solution)/shard_map/scatter-add | solution.py:48
  21.6 72.0 %all-reduce.4.cloned.1.call-done = f32[16384]{0:T(1024)} async-done(((f32[16384]{0:T(1024)}), f32[16384]{0:T(1024)}) %all-reduce.4.cloned.1.call-update) | async-done | bytes 65552 | tf_op jit(solution)/shard_map/psum | solution.py:51
  93.5 0.9 subtract_multiply_fusion.1
  94.4 11.8 %gather_fusion.1 = f32[2048]{0:T(1024)S(1)} fusion(f32[16384]{0:T(1024)S(1)} %subtract_multiply_fusion.1, s32[2048]{0:T(1024)S(1)} %broadcast_clamp_fusion), kind=kCustom, calls=%fused_computation.1 | custom fusion | bytes 24576 | tf_op jit(solution)/shard_map/gather | solution.py:60
  106.3 13.1 %gather_fusion = bf16[2048]{0:T(1024)(128)(2,1)S(1)} fusion(bf16[16384]{0:T(1024)(128)(2,1)S(1)} %fusion.35, s32[2048]{0:T(1024)S(1)} %broadcast_clamp_fusion), kind=kCustom, calls=%fused_computation | custom fusion | bytes 16384 | tf_op jit(solution)/shard_map/gather | solution.py:55
  119.7 0.9 fusion.9
  120.6 0.7 fusion.59
  121.7 0.7 fusion.57
  122.8 0.7 fusion.55
  124.1 11.8 %scatter_custom_fusion.1 = f32[16384]{0:T(1024)} fusion(s32[2048]{0:T(1024)S(1)} %bitcast.147, f32[2048]{0:T(1024)S(1)} %bitcast.148, f32[]{:T(128)} %constant.9.clone.1), kind=kCustom, calls=%fused_computation.34 | custom fusion | flops 2048 | bytes 65540 | tf_op jit(solution)/shard_map/scatter-add | solution.py:48
  135.9 69.3 %all-reduce.6.cloned.1.call-done = f32[16384]{0:T(1024)} async-done(((f32[16384]{0:T(1024)}), f32[16384]{0:T(1024)}) %all-reduce.6.cloned.1.call-update) | async-done | bytes 65552 | tf_op jit(solution)/shard_map/psum | solution.py:51
  205.3 0.9 fusion.36
  206.2 13.1 %gather_fusion.2 = bf16[2048]{0:T(1024)(128)(2,1)S(1)} fusion(bf16[16384]{0:T(1024)(128)(2,1)S(1)} %fusion.36, s32[2048]{0:T(1024)S(1)} %broadcast_clamp_fusion), kind=kCustom, calls=%fused_computation.2 | custom fusion | bytes 16384 | tf_op jit(solution)/shard_map/gather | solution.py:55
  219.3 11.8 %gather_fusion.3 = f32[2048]{0:T(1024)S(1)} fusion(f32[16384]{0:T(1024)S(1)} %subtract_multiply_fusion, s32[2048]{0:T(1024)S(1)} %broadcast_clamp_fusion), kind=kCustom, calls=%fused_computation.3 | custom fusion | bytes 24576 | tf_op jit(solution)/shard_map/gather | solution.py:60
  231.3 0.9 fusion.15
  232.3 0.7 fusion.52
  233.4 0.7 fusion.50
  234.5 0.7 fusion.48
  235.3 5.7 %psum.37 = f32[4,256]{1,0:T(4,128)S(1)} all-reduce(f32[4,256]{1,0:T(4,128)S(1)} %get-tuple-element.13), channel_id=1, replica_groups=mesh['feat'=8,'row'=2,'col'=2] {'row','col'}, use_global_device_ids=true, to_apply=%region_16.0 | all-reduce | flops 1024 | bytes 8192 | tf_op jit(solution)/shard_map/psum | solution.py:69
  241.0 0.7 multiply_reduce_fusion.1
  241.7 0.6 subtract_bitcast_fusion
  243.0 40.8 %all-reduce = (f32[]{:T(128)}, f32[]{:T(128)}) all-reduce(f32[]{:T(128)S(6)} %div.99, f32[]{:T(128)} %get-tuple-element.4), channel_id=1, replica_groups=mesh['feat'=8,'row'=2,'col'=2] {'feat','row','col'}, use_global_device_ids=true, to_apply=%region_20.0 | all-reduce | flops 2 | bytes 16 | tf_op jit(solution)/shard_map/psum | solution.py:74
  (72 shorter events, 3.9 us)
Async XLA Ops:
  7.2 2.4 copy-start.7
  7.2 14.3 %copy-start.3 = (s32[1,16384]{1,0:T(1,128)S(1)}, s32[1,16384]{1,0:T(1,128)}, u32[]{:S(2)}) copy-start(s32[1,16384]{1,0:T(1,128)} %param.11) | copy-start | bytes 196612
  7.2 86.4 %all-reduce.4.cloned.1.call-start = ((), (), s32[]{:S(2)}) async-start(), calls=%async_computation | async-start | bytes 131072 | tf_op jit(solution)/shard_map/psum | solution.py:51
  21.4 183.9 %all-reduce.6.cloned.1.call-start = ((), (), s32[]{:S(2)}) async-start(), calls=%async_computation.1 | async-start | bytes 131072 | tf_op jit(solution)/shard_map/psum | solution.py:51
  94.4 11.8 %copy-start.1 = (f32[16384]{0:T(1024)S(1)}, f32[16384]{0:T(1024)}, u32[]{:S(2)}) copy-start(f32[16384]{0:T(1024)} %all-reduce.4.cloned.1.call-done) | copy-start | bytes 196612
  106.3 13.1 %copy-start = (bf16[1,4,512,256]{3,2,1,0:T(8,128)(2,1)S(1)}, bf16[1,4,512,256]{3,2,1,0:T(8,128)(2,1)}, u32[]{:S(2)}) copy-start(bf16[1,4,512,256]{3,2,1,0:T(8,128)(2,1)} %param.9) | copy-start | bytes 3145732
  119.6 0.9 copy-start.4
  119.6 1.0 copy-start.5
  119.6 1.0 copy-start.6
  206.1 13.1 %copy-start.2 = (f32[16384]{0:T(1024)S(1)}, f32[16384]{0:T(1024)}, u32[]{:S(2)}) copy-start(f32[16384]{0:T(1024)} %all-reduce.6.cloned.1.call-done) | copy-start | bytes 196612
  235.3 50.3 %copy-start.9 = (f32[4,256]{1,0:T(4,128)}, f32[4,256]{1,0:T(4,128)S(1)}, u32[]{:S(2)}) copy-start(f32[4,256]{1,0:T(4,128)S(1)} %get-tuple-element.14) | copy-start | bytes 12292
  241.7 44.0 %copy-start.8 = (f32[4,256]{1,0:T(4,128)}, f32[4,256]{1,0:T(4,128)S(1)}, u32[]{:S(2)}) copy-start(f32[4,256]{1,0:T(4,128)S(1)} %get-tuple-element.12) | copy-start | bytes 12292
Sparse Core Ops, SparseCore 0:
  21.5 71.9 all-reduce.3
  136.0 69.1 all-reduce.5
where the time goes:
time: 293 us; the launch traced here: 292 us
  waiting for transfers between devices  141 us (48%)
  local copies, waits for them, and re-layouts  49.8 us (17%)
  blocking collectives  46.4 us (16%)
  other arithmetic  30.1 us (10%)
  between operations  16.4 us (6%)
  matrix products  8.28 us (3%)
    psum x2, waiting for transfers between devices, local(): margins = lax.psum(local_margins, 'feat')  141 us
    psum x1, blocking collectives, local(): lax.psum((primal_local, change_local / jnp.float32(shards)), ('feat', 'ro...  40.8 us
    gather x2, local copies, waits for them, and re-layouts, local(): misfit_rows = misfit[index_rows].astype(jnp.bfloat16)  26.2 us
    scatter-add x2, other arithmetic, local(): jax.ops.segment_sum(partial_value.reshape(-1), flat_index, num_segments=s...  23.7 us
    gather x4, local copies, waits for them, and re-layouts, local(): weights[index_rows][:, :, None]  23.6 us
  transfers between devices with their start and end apart: 2, of which 2 were waited for; matrix products, arithmetic and copies ran while one was open for 0% of the time, Pallas kernels for 0%

commit v1 on v0

--- a/solution.py
+++ b/solution.py
@@ -48,7 +48,7 @@
         local_margins = jax.ops.segment_sum(
             partial_value.reshape(-1), flat_index, num_segments=samples
         )
-        margins = lax.psum(local_margins, "feat")
+        margins = jnp.sum(lax.all_gather(local_margins, "feat"), axis=0)
         prob = jax.nn.sigmoid(margins)
         misfit = prob - targets
         weights = prob * (1.0 - prob)

time: 293 us -> 200 us (0.68)
  waiting for transfers between devices: 141 us -> 0 us
  blocking collectives: 46.4 us -> 110 us
  between operations: 16.4 us -> 2.92 us
    psum x2 -> x0, waiting for transfers between devices: 141 us -> none  [local(): margins = lax.psum(local_margins, 'feat')]
    all_gather x0 -> x2, blocking collectives: none -> 64.3 us  [local(): margins = jnp.sum(lax.all_gather(local_margins, 'feat'), axis=0)]
  transfers between devices with their start and end apart: 2 -> 0, of which waited for: 2 -> 0; matrix products, arithmetic and copies ran while one was open for 0% -> 0% of each run, Pallas kernels for 0% -> 0%
where the time goes in v1:
time: 200 us; the launch traced here: 199 us
  blocking collectives  110 us (55%)
  local copies, waits for them, and re-layouts  50.4 us (25%)
  other arithmetic  27.6 us (14%)
  matrix products  8.27 us (4%)
  between operations  2.92 us (1%)
    all_gather x2, blocking collectives, local(): margins = jnp.sum(lax.all_gather(local_margins, 'feat'), axis=0)  64.3 us
    psum x1, blocking collectives, local(): lax.psum((primal_local, change_local / jnp.float32(shards)), ('feat', 'ro...  40.3 us
    gather x2, local copies, waits for them, and re-layouts, local(): misfit_rows = misfit[index_rows].astype(jnp.bfloat16)  26.2 us
    gather x4, local copies, waits for them, and re-layouts, local(): weights[index_rows][:, :, None]  23.6 us
    scatter-add x2, other arithmetic, local(): jax.ops.segment_sum(partial_value.reshape(-1), flat_index, num_segments=s...  22.6 us
    psum x1, blocking collectives, local(): totals = lax.psum(combined, ('row', 'col'))  5.65 us

profile of v1, /device:TPU:0, one launch (start us, length us, event | category | flops | bytes accessed | tf_op | source)
XLA Modules:
  0.0 199.4 jit_solution(2603117349400876578)
XLA Ops:
  0.7 0.7 fusion.62
  1.4 1.6 fusion.26
  3.0 11.3 %scatter_custom_fusion = f32[16384]{0:T(1024)S(1)} fusion(s32[2048]{0:T(1024)S(1)} %bitcast.146, f32[2048]{0:T(1024)S(1)} %bitcast.148, f32[]{:T(128)} %constant.9.clone.1), kind=kCustom, calls=%fused_computation.36 | custom fusion | flops 2048 | bytes 65540 | tf_op jit(solution)/shard_map/scatter-add | solution.py:48
  14.4 33.0 %all-gather = f32[131072]{0:T(1024)S(1)} all-gather(f32[16384]{0:T(1024)S(1)} %scatter_custom_fusion), channel_id=2, replica_groups=mesh['feat'=8,'row'=2,'col'=2] {'feat'}, dimensions={0}, use_global_device_ids=true | all-gather | bytes 589824 | tf_op jit(solution)/shard_map/all_gather | solution.py:51
  47.7 13.1 %gather_fusion = bf16[2048]{0:T(1024)(128)(2,1)S(1)} fusion(bf16[16384]{0:T(1024)(128)(2,1)S(1)} %fusion.35, s32[2048]{0:T(1024)S(1)} %broadcast_clamp_fusion), kind=kCustom, calls=%fused_computation | custom fusion | bytes 16384 | tf_op jit(solution)/shard_map/gather | solution.py:55
  60.9 11.8 %gather_fusion.1 = f32[2048]{0:T(1024)S(1)} fusion(f32[16384]{0:T(1024)S(1)} %subtract_multiply_fusion.1, s32[2048]{0:T(1024)S(1)} %broadcast_clamp_fusion), kind=kCustom, calls=%fused_computation.1 | custom fusion | bytes 24576 | tf_op jit(solution)/shard_map/gather | solution.py:60
  73.4 0.9 fusion.9
  74.3 0.7 fusion.59
  75.4 0.7 fusion.57
  76.5 0.7 fusion.55
  77.4 0.4 fusion.20
  77.7 11.3 %scatter_custom_fusion.1 = f32[16384]{0:T(1024)S(1)} fusion(s32[2048]{0:T(1024)S(1)} %bitcast.147, f32[2048]{0:T(1024)S(1)} %bitcast.149, f32[]{:T(128)} %constant.9.clone.1), kind=kCustom, calls=%fused_computation.34 | custom fusion | flops 2048 | bytes 65540 | tf_op jit(solution)/shard_map/scatter-add | solution.py:48
  89.0 31.3 %all-gather.1 = f32[131072]{0:T(1024)S(1)} all-gather(f32[16384]{0:T(1024)S(1)} %scatter_custom_fusion.1), channel_id=3, replica_groups=mesh['feat'=8,'row'=2,'col'=2] {'feat'}, dimensions={0}, use_global_device_ids=true | all-gather | bytes 589824 | tf_op jit(solution)/shard_map/all_gather | solution.py:51
  120.6 13.1 %gather_fusion.2 = bf16[2048]{0:T(1024)(128)(2,1)S(1)} fusion(bf16[16384]{0:T(1024)(128)(2,1)S(1)} %fusion.36, s32[2048]{0:T(1024)S(1)} %broadcast_clamp_fusion), kind=kCustom, calls=%fused_computation.2 | custom fusion | bytes 16384 | tf_op jit(solution)/shard_map/gather | solution.py:55
  133.7 11.8 %gather_fusion.3 = f32[2048]{0:T(1024)S(1)} fusion(f32[16384]{0:T(1024)S(1)} %subtract_multiply_fusion, s32[2048]{0:T(1024)S(1)} %broadcast_clamp_fusion), kind=kCustom, calls=%fused_computation.3 | custom fusion | bytes 24576 | tf_op jit(solution)/shard_map/gather | solution.py:60
  145.8 0.9 fusion.15
  146.7 0.7 fusion.52
  147.8 0.7 fusion.50
  148.9 0.7 fusion.48
  149.8 5.7 %psum.21 = f32[4,256]{1,0:T(4,128)S(1)} all-reduce(f32[4,256]{1,0:T(4,128)S(1)} %get-tuple-element.13), channel_id=1, replica_groups=mesh['feat'=8,'row'=2,'col'=2] {'row','col'}, use_global_device_ids=true, to_apply=%region_16.0 | all-reduce | flops 1024 | bytes 8192 | tf_op jit(solution)/shard_map/psum | solution.py:69
  155.4 0.6 multiply_reduce_fusion.1
  156.7 0.6 subtract_bitcast_fusion
  157.3 40.3 %all-reduce = (f32[]{:T(128)}, f32[]{:T(128)}) all-reduce(f32[]{:T(128)S(6)} %div.99, f32[]{:T(128)} %get-tuple-element.4), channel_id=1, replica_groups=mesh['feat'=8,'row'=2,'col'=2] {'feat','row','col'}, use_global_device_ids=true, to_apply=%region_20.0 | all-reduce | flops 2 | bytes 16 | tf_op jit(solution)/shard_map/psum | solution.py:74
  198.8 0.6 pad_maximum_fusion
  (68 shorter events, 3.7 us)
Async XLA Ops:
  0.6 2.4 %copy-start.5 = (s32[1,4,512]{2,1,0:T(4,128)S(1)}, s32[1,4,512]{2,1,0:T(4,128)}, u32[]{:S(2)}) copy-start(s32[1,4,512]{2,1,0:T(4,128)} %param.10) | copy-start | bytes 24580
  0.6 13.7 %copy-start.1 = (s32[1,16384]{1,0:T(1,128)S(1)}, s32[1,16384]{1,0:T(1,128)}, u32[]{:S(2)}) copy-start(s32[1,16384]{1,0:T(1,128)} %param.11) | copy-start | bytes 196612
  60.9 11.9 %copy-start = (bf16[1,4,512,256]{3,2,1,0:T(8,128)(2,1)S(1)}, bf16[1,4,512,256]{3,2,1,0:T(8,128)(2,1)}, u32[]{:S(2)}) copy-start(bf16[1,4,512,256]{3,2,1,0:T(8,128)(2,1)} %param.9) | copy-start | bytes 3145732
  72.7 0.7 copy-start.2
  72.7 0.7 copy-start.3
  72.7 0.7 copy-start.4
  149.8 49.7 %copy-start.7 = (f32[4,256]{1,0:T(4,128)}, f32[4,256]{1,0:T(4,128)S(1)}, u32[]{:S(2)}) copy-start(f32[4,256]{1,0:T(4,128)S(1)} %get-tuple-element.14) | copy-start | bytes 12292
  156.0 43.4 %copy-start.6 = (f32[4,256]{1,0:T(4,128)}, f32[4,256]{1,0:T(4,128)S(1)}, u32[]{:S(2)}) copy-start(f32[4,256]{1,0:T(4,128)S(1)} %get-tuple-element.12) | copy-start | bytes 12292
